TPU v7x, 32 devices: a whole 2x2x4 slice. The times are simulated.
32 devices in a mesh: tab: 8 (over z, x), rep: 4 (over y, core).
Axes of the slice: x: 2, y: 2, z: 4, core: 2. Of those that a mesh axis runs over, the one named last changes fastest.
Arguments:
- sample_ids: int32 [16384, 26], P(('tab', 'rep')), may hold values from 0 to 4095, as said below
- features: bfloat16 [16384, 27, 128], P(('tab', 'rep')), may hold values from -6 to 6
- pair_grad: bfloat16 [351, 16384], P(None, ('tab', 'rep')), may hold values from -1.59375 to 1.59375
Outputs:
- table_grad: float32 [26, 4096, 128], P(None, ('tab', 'rep'))
- dense_grad: float32 [16384, 128], P(('tab', 'rep'))
Inputs may be any that keep to these rules, and one draw needn't show every extreme that they name: `sample_ids`: row r is owned by device r // 128, numbered tab * 4 + rep. For each field and the 512 samples of one device (aligned blocks of rows in device order), at most 32 ids fall in the rows of any one device, and at most 128 in the rows of any one tab index; in every block and field both bounds are reached.
All inputs are finite; a program needn't handle non-finite values.
Results may differ from a plain program's by a relative error of at most 0.0029.
Values may be sent and summed in bfloat16 or wider, within the bound.
No kernel may reach another device: no remote copies, remote signals or barrier semaphores. Data moves between devices by JAX's collectives and lax.ppermute only.
A program may use at most 128 MiB of HBM per device.

v0:
```python
import jax
import jax.numpy as jnp
import numpy as np
from jax import lax
from jax.sharding import PartitionSpec as P

RQ = 128


def pair_table(vectors):
    row_of, col_of = np.tril_indices(vectors, -1)
    spread = np.zeros((row_of.shape[0], vectors * vectors), np.float32)
    places = np.arange(row_of.shape[0])
    spread[places, row_of * vectors + col_of] = 1.0
    spread[places, col_of * vectors + row_of] = 1.0
    return spread


def arrival_order(targets, bins):
    matches = (targets[:, None] == jnp.arange(bins, dtype=jnp.int32)[None, :]).astype(jnp.int32)
    return jnp.sum(jnp.cumsum(matches, axis=0) * matches, axis=1) - 1


def place_field(slot_of, tag_of, grads, slot_total):
    placing = jnp.arange(slot_total, dtype=jnp.int32)[:, None] == slot_of[None, :]
    placed = jnp.dot(
        placing.astype(jnp.bfloat16), grads, preferred_element_type=jnp.float32
    ).astype(jnp.bfloat16)
    shifted = (tag_of + 1).astype(jnp.float32)
    tag_sum = jnp.dot(placing.astype(jnp.float32), shifted, precision=lax.Precision.HIGHEST)
    return (placed, tag_sum.astype(jnp.int32) - 1)


def tally_rows(arrived, row_tags, row_count):

    def per_field(pieces):
        slot_grads, slot_tags = pieces
        matches = (slot_tags[None, :] == jnp.arange(row_count, dtype=jnp.int32)[:, None]).astype(
            jnp.bfloat16
        )
        return jnp.dot(matches, slot_grads, preferred_element_type=jnp.float32)

    return lax.map(per_field, (arrived, row_tags))


def local(sample_ids, features, pair_grad):
    vectors = features.shape[1]
    samples = features.shape[0]
    depth = features.shape[2]
    spread = jnp.asarray(pair_table(vectors).T).astype(jnp.bfloat16)
    symmetric = jnp.dot(spread, pair_grad, preferred_element_type=jnp.float32)
    symmetric = symmetric.astype(jnp.bfloat16).reshape(vectors, vectors, samples)
    gradients = jnp.einsum("fgb,bge->fbe", symmetric, features, preferred_element_type=jnp.float32)
    dense_grad = gradients[0]
    field_grads = gradients[1:].astype(jnp.bfloat16)
    fields = vectors - 1
    col_count = lax.axis_size("tab")
    rep_count = lax.axis_size("rep")
    capacity = 2 * samples // (col_count * rep_count)
    slot_total = col_count * rep_count * capacity
    ids_by_field = sample_ids.T

    def build_owner(pieces):
        column_ids, grads = pieces
        owners = column_ids // RQ
        slot_of = owners * capacity + arrival_order(owners, col_count * rep_count)
        return place_field(slot_of, column_ids % RQ, grads, slot_total)

    outgoing, row_tags = lax.map(build_owner, (ids_by_field, field_grads))
    outgoing = outgoing.reshape(fields, col_count, rep_count, capacity, depth)
    row_tags = row_tags.reshape(fields, col_count, rep_count, capacity)
    arrived, tags_in = (
        lax.all_to_all(
            lax.all_to_all(outgoing, "tab", split_axis=1, concat_axis=1, tiled=True),
            "rep",
            split_axis=2,
            concat_axis=2,
            tiled=True,
        ),
        lax.all_to_all(
            lax.all_to_all(row_tags, "tab", split_axis=1, concat_axis=1, tiled=True),
            "rep",
            split_axis=2,
            concat_axis=2,
            tiled=True,
        ),
    )
    table_grad = tally_rows(arrived.reshape(fields, -1, depth), tags_in.reshape(fields, -1), RQ)
    return (table_grad, dense_grad)


def solution(mesh):
    placed = (P(("tab", "rep"), None), P(("tab", "rep"), None, None), P(None, ("tab", "rep")))
    return jax.shard_map(
        local,
        mesh=mesh,
        in_specs=placed,
        out_specs=(P(None, ("tab", "rep"), None), P(("tab", "rep"), None)),
        check_vma=False,
    )
```

profile of v0, /device:TPU:0, one launch (start us, length us, event | category | flops | bytes accessed | tf_op | source)
XLA Modules:
  0.0 536.2 jit_solution(541020844716352694)
XLA Ops:
  0.7 2.7 convolution_convert_fusion
  3.4 2.2 reshape.112
  5.6 7.5 %copy.20 = bf16[27,27,512]{1,0,2:T(8,128)(2,1)} copy(bf16[27,27,512]{2,1,0:T(8,128)(2,1)} %reshape.112) | data formatting | bytes 1492992 | tf_op jit(solution)/shard_map/reshape | solution.py:52
  13.1 4.5 fusion.25
  18.8 2.1 copy-done.2
  22.2 173.3 %while.25 = (s32[]{:T(128)}, bf16[26,1024,128]{2,1,0:T(8,128)(2,1)}, s32[26,1024]{1,0:T(8,128)}, s32[26,512]{1,0:T(8,128)}, bf16[26,512,128]{2,1,0:T(8,128)(2,1)S(1)}, /*index=5*/s32[]{:T(128)}, s32[]{:T(128)}) while((s32[]{:T(128)}, bf16[26,1024,128]{2,1,0:T(8,128)(2,1)}, s32[26,1024]{1,0:T(8,128)}, s32[26,512]{1,0:T(8,128)}, ...), condition=%wide.region_4.5_spmd, body=%wide.region_0.4_spmd.sunk | while | flops 143897568 | bytes 717545 | solution.py:69
  197.7 7.2 %all-to-all-start = ((s32[8,1,3328]{2,1,0:T(1,128)}), s32[8,1,3328]{2,1,0:T(1,128)S(1)}, u32[]{:S(2)}, u32[]{:S(2)}) async-start(s32[8,1,3328]{2,1,0:T(1,128)} %reshape.120), calls=%async_computation | async-start | bytes 212992 | tf_op jit(solution)/shard_map/all_to_all | solution.py:81
  205.0 8.6 %copy.26 = bf16[26,8,4,32,128]{4,3,2,0,1:T(8,128)(2,1)} copy(bf16[26,8,4,32,128]{4,3,2,1,0:T(8,128)(2,1)} %bitcast.88) | data formatting | bytes 13631488 | tf_op jit(solution)/shard_map/reshape | solution.py:70
  213.6 6.0 %all-to-all-start.2 = ((bf16[26,8,4,32,128]{4,3,2,0,1:T(8,128)(2,1)}), bf16[26,8,4,32,128]{4,3,2,0,1:T(8,128)(2,1)}, u32[]{:S(2)}, u32[]{:S(2)}) async-start(bf16[26,8,4,32,128]{4,3,2,0,1:T(8,128)(2,1)} %copy.26), calls=%async_computation.2 | async-start | bytes 13631488 | tf_op jit(solution)/shard_map/all_to_all | solution.py:74
  222.2 146.3 %all-to-all-done.2 = bf16[26,8,4,32,128]{4,3,2,0,1:T(8,128)(2,1)} async-done(((bf16[26,8,4,32,128]{4,3,2,0,1:T(8,128)(2,1)}), bf16[26,8,4,32,128]{4,3,2,0,1:T(8,128)(2,1)}, u32[]{:S(2)}, u32[]{:S(2)}) %all-to-all-start.2) | async-done | bytes 6815776 | tf_op jit(solution)/shard_map/all_to_all | solution.py:74
  368.5 3.5 all-to-all-start.1
  372.0 7.9 %copy.27 = bf16[26,8,4,32,128]{4,3,1,0,2:T(8,128)(2,1)} copy(bf16[26,8,4,32,128]{4,3,2,0,1:T(8,128)(2,1)} %all-to-all-done.2) | data formatting | bytes 13631488 | tf_op jit(solution)/shard_map/all_to_all | solution.py:74
  379.8 5.4 %all-to-all-start.3 = ((bf16[26,8,4,32,128]{4,3,1,0,2:T(8,128)(2,1)}), bf16[26,8,4,32,128]{4,3,1,0,2:T(8,128)(2,1)}, u32[]{:S(2)}, u32[]{:S(2)}) async-start(bf16[26,8,4,32,128]{4,3,1,0,2:T(8,128)(2,1)} %copy.27), calls=%async_computation.3 | async-start | bytes 13631488 | tf_op jit(solution)/shard_map/all_to_all | solution.py:73
  385.3 2.4 slice.25
  389.9 71.6 %all-to-all-done.3 = bf16[26,8,4,32,128]{4,3,1,0,2:T(8,128)(2,1)} async-done(((bf16[26,8,4,32,128]{4,3,1,0,2:T(8,128)(2,1)}), bf16[26,8,4,32,128]{4,3,1,0,2:T(8,128)(2,1)}, u32[]{:S(2)}, u32[]{:S(2)}) %all-to-all-start.3) | async-done | bytes 6815776 | tf_op jit(solution)/shard_map/all_to_all | solution.py:73
  461.6 8.0 %copy.28 = bf16[26,8,4,32,128]{4,3,2,1,0:T(8,128)(2,1)} copy(bf16[26,8,4,32,128]{4,3,1,0,2:T(8,128)(2,1)} %all-to-all-done.3) | data formatting | bytes 13631488 | tf_op jit(solution)/shard_map/all_to_all | solution.py:73
  469.6 66.7 %while.26 = (s32[]{:T(128)}, f32[26,128,128]{2,1,0:T(8,128)}, s32[26,1024]{1,0:T(8,128)}, bf16[26,1024,128]{2,1,0:T(8,128)(2,1)}, s32[]{:T(128)}) while((s32[]{:T(128)}, f32[26,128,128]{2,1,0:T(8,128)}, s32[26,1024]{1,0:T(8,128)}, bf16[26,1024,128]{2,1,0:T(8,128)(2,1)}, s32[]{:T(128)}) %tuple.59), condition=%wide.region_6.7_spmd, body=%wide.region_5.6_spmd.sunk | while | flops 33685504 | bytes 341065 | solution.py:43
  470.3 1.8 fusion.49
  472.9 1.8 fusion.49
  480.6 1.8 fusion.49
  483.1 1.8 fusion.49
  485.7 1.8 fusion.49
  490.8 1.8 fusion.49
  493.4 1.8 fusion.49
  501.1 1.8 fusion.49
  503.7 1.8 fusion.49
  506.2 1.8 fusion.49
  511.3 1.8 fusion.49
  521.6 1.8 fusion.49
  524.2 1.8 fusion.49
  526.7 1.8 fusion.49
  531.9 1.8 fusion.49
  (451 shorter events, 221.7 us)
Async XLA Ops:
  0.6 12.5 %copy-start = (bf16[512,27,128]{2,0,1:T(8,128)(2,1)S(1)}, bf16[512,27,128]{2,0,1:T(8,128)(2,1)}, u32[]{:S(2)}) copy-start(bf16[512,27,128]{2,0,1:T(8,128)(2,1)} %param.9) | copy-start | bytes 10616836
  17.7 3.2 copy-start.2
  197.7 15.9 %all-to-all-start = ((s32[8,1,3328]{2,1,0:T(1,128)}), s32[8,1,3328]{2,1,0:T(1,128)S(1)}, u32[]{:S(2)}, u32[]{:S(2)}) async-start(s32[8,1,3328]{2,1,0:T(1,128)} %reshape.120), calls=%async_computation | async-start | bytes 212992 | tf_op jit(solution)/shard_map/all_to_all | solution.py:81
  213.6 154.9 %all-to-all-start.2 = ((bf16[26,8,4,32,128]{4,3,2,0,1:T(8,128)(2,1)}), bf16[26,8,4,32,128]{4,3,2,0,1:T(8,128)(2,1)}, u32[]{:S(2)}, u32[]{:S(2)}) async-start(bf16[26,8,4,32,128]{4,3,2,0,1:T(8,128)(2,1)} %copy.26), calls=%async_computation.2 | async-start | bytes 13631488 | tf_op jit(solution)/shard_map/all_to_all | solution.py:74
  368.5 11.4 %all-to-all-start.1 = ((s32[4,1,6656]{2,1,0:T(1,128)}), s32[4,1,6656]{2,1,0:T(1,128)S(1)}, u32[]{:S(2)}, u32[]{:S(2)}) async-start(s32[4,1,6656]{2,1,0:T(1,128)} %reshape.122), calls=%async_computation.1 | async-start | bytes 212992 | tf_op jit(solution)/shard_map/all_to_all | solution.py:80
  379.8 81.7 %all-to-all-start.3 = ((bf16[26,8,4,32,128]{4,3,1,0,2:T(8,128)(2,1)}), bf16[26,8,4,32,128]{4,3,1,0,2:T(8,128)(2,1)}, u32[]{:S(2)}, u32[]{:S(2)}) async-start(bf16[26,8,4,32,128]{4,3,1,0,2:T(8,128)(2,1)} %copy.27), calls=%async_computation.3 | async-start | bytes 13631488 | tf_op jit(solution)/shard_map/all_to_all | solution.py:73
  461.5 74.7 %copy-start.1 = (bf16[512,27,128]{2,0,1:T(8,128)(2,1)S(1)}, bf16[512,27,128]{2,0,1:T(8,128)(2,1)}, u32[]{:S(2)}) copy-start(bf16[512,27,128]{2,0,1:T(8,128)(2,1)} %param.9) | copy-start | bytes 10616836
where the time goes:
time: 544 us; the launch traced here: 536 us
  waiting for transfers between devices  218 us (40%)
  local copies, waits for them, and re-layouts  128 us (24%)
  matrix products  111 us (20%)
  other arithmetic  56.4 us (10%)
  starting transfers between devices  22.1 us (4%)
    all_to_all x1, waiting for transfers between devices, local(): lax.all_to_all(outgoing, 'tab', split_axis=1, concat_axis=1, tiled=True)  146 us
    all_to_all x1, waiting for transfers between devices, local(): lax.all_to_all(lax.all_to_all(outgoing, 'tab', split_axis=1, concat_axis=...  71.6 us
    dot_general x26, matrix products, per_field(): return jnp.dot(matches, slot_grads, preferred_element_type=jnp.float32)  46.8 us
    dynamic_update_slice x26, local copies, waits for them, and re-layouts, local(): outgoing, row_tags = lax.map(build_owner, (ids_by_field, field_grads))  36.6 us
    another operation x52, other arithmetic  31.3 us
    dot_general x26, matrix products, place_field(): jnp.dot(placing.astype(jnp.bfloat16), grads, preferred_element_type=jnp.f...  30.5 us
    dot_general x26, matrix products, place_field(): jnp.dot(placing.astype(jnp.float32), shifted, precision=lax.Precision.HIG...  26.3 us
    dynamic_slice x26, local copies, waits for them, and re-layouts, tally_rows(): return lax.map(per_field, (arrived, row_tags))  19.9 us
  transfers between devices with their start and end apart: 4, of which 2 were waited for; matrix products, arithmetic and copies ran while one was open for 4% of the time, Pallas kernels for 0%

commit v1 on v0

--- a/solution.py
+++ b/solution.py
@@ -1,3 +1,4 @@
+import functools
 import jax
 import jax.numpy as jnp
 import numpy as np
@@ -5,6 +6,21 @@
 from jax.sharding import PartitionSpec as P
 
 RQ = 128
+
+
+def test_units(s0, axis_k, on_dim):
+    return jnp.concatenate(
+        lax.all_to_all(
+            jnp.stack(jnp.split(s0, lax.axis_size("tab"), axis_k), axis=0),
+            "tab",
+            split_axis=0,
+            concat_axis=0,
+        ),
+        on_dim,
+    )
+
+
+track_knots_here = functools.partial(test_units, axis_k=1, on_dim=1)
 
 
 def pair_table(vectors):
@@ -70,13 +86,7 @@
     outgoing = outgoing.reshape(fields, col_count, rep_count, capacity, depth)
     row_tags = row_tags.reshape(fields, col_count, rep_count, capacity)
     arrived, tags_in = (
-        lax.all_to_all(
-            lax.all_to_all(outgoing, "tab", split_axis=1, concat_axis=1, tiled=True),
-            "rep",
-            split_axis=2,
-            concat_axis=2,
-            tiled=True,
-        ),
+        lax.all_to_all(track_knots_here(outgoing), "rep", split_axis=2, concat_axis=2, tiled=True),
         lax.all_to_all(
             lax.all_to_all(row_tags, "tab", split_axis=1, concat_axis=1, tiled=True),
             "rep",

time: 544 us -> 547 us (level)
    unnamed x10 -> x19, local copies, waits for them, and re-layouts: 4.29 us -> 14.8 us
    all_to_all x2 -> x1, local copies, waits for them, and re-layouts: 15.9 us -> 7.86 us  [local(): lax.all_to_all(track_knots_here(outgoing), 'rep', split_axis=2, concat_ax...]
  transfers between devices with their start and end apart: 4 -> 4, of which waited for: 2 -> 2; matrix products, arithmetic and copies ran while one was open for 4% -> 6% of each run, Pallas kernels for 0% -> 0%
where the time goes in v1:
time: 547 us; the launch traced here: 539 us
  waiting for transfers between devices  216 us (39%)
  local copies, waits for them, and re-layouts  132 us (24%)
  matrix products  111 us (20%)
  other arithmetic  56.4 us (10%)
  starting transfers between devices  22.1 us (4%)
    all_to_all x1, waiting for transfers between devices, test_units(): lax.all_to_all(jnp.stack(jnp.split(s0, lax.axis_size('tab'), axis_k), axi...  146 us
    all_to_all x1, waiting for transfers between devices, local(): lax.all_to_all(track_knots_here(outgoing), 'rep', split_axis=2, concat_ax...  69.7 us
    dot_general x26, matrix products, per_field(): return jnp.dot(matches, slot_grads, preferred_element_type=jnp.float32)  46.8 us
    dynamic_update_slice x26, local copies, waits for them, and re-layouts, local(): outgoing, row_tags = lax.map(build_owner, (ids_by_field, field_grads))  36.6 us
    another operation x52, other arithmetic  31.3 us
    dot_general x26, matrix products, place_field(): jnp.dot(placing.astype(jnp.bfloat16), grads, preferred_element_type=jnp.f...  30.5 us
    dot_general x26, matrix products, place_field(): jnp.dot(placing.astype(jnp.float32), shifted, precision=lax.Precision.HIG...  26.3 us
    dynamic_slice x26, local copies, waits for them, and re-layouts, tally_rows(): return lax.map(per_field, (arrived, row_tags))  19.9 us
  transfers between devices with their start and end apart: 4, of which 2 were waited for; matrix products, arithmetic and copies ran while one was open for 6% of the time, Pallas kernels for 0%

profile of v1, /device:TPU:0, one launch (start us, length us, event | category | flops | bytes accessed | tf_op | source)
XLA Modules:
  0.0 539.1 jit_solution(4381882990473123766)
XLA Ops:
  0.7 2.7 convolution_convert_fusion
  3.4 2.2 reshape.118
  5.6 7.5 %copy.36 = bf16[27,27,512]{1,0,2:T(8,128)(2,1)} copy(bf16[27,27,512]{2,1,0:T(8,128)(2,1)} %reshape.118) | data formatting | bytes 1492992 | tf_op jit(solution)/shard_map/reshape | solution.py:68
  13.1 4.5 fusion.25
  20.9 173.3 %while.25 = (s32[]{:T(128)}, bf16[26,1024,128]{2,1,0:T(8,128)(2,1)}, s32[26,1024]{1,0:T(8,128)}, s32[26,512]{1,0:T(8,128)}, bf16[26,512,128]{2,1,0:T(8,128)(2,1)S(1)}, /*index=5*/s32[]{:T(128)}, s32[]{:T(128)}) while((s32[]{:T(128)}, bf16[26,1024,128]{2,1,0:T(8,128)(2,1)}, s32[26,1024]{1,0:T(8,128)}, s32[26,512]{1,0:T(8,128)}, ...), condition=%wide.region_4.5_spmd, body=%wide.region_0.4_spmd.sunk | while | flops 143897568 | bytes 717545 | solution.py:85
  196.4 7.2 %all-to-all-start = ((s32[8,1,3328]{2,1,0:T(1,128)}), s32[8,1,3328]{2,1,0:T(1,128)S(1)}, u32[]{:S(2)}, u32[]{:S(2)}) async-start(s32[8,1,3328]{2,1,0:T(1,128)} %reshape.128), calls=%async_computation | async-start | bytes 212992 | tf_op jit(solution)/shard_map/all_to_all | solution.py:91
  203.6 2.3 fusion.35
  205.9 2.3 fusion.34
  208.2 2.2 fusion.33
  210.4 2.2 fusion.32
  216.5 6.0 %all-to-all-start.2 = ((bf16[8,26,1,4,32,128]{5,4,3,1,2,0:T(8,128)(2,1)}), bf16[8,26,1,4,32,128]{5,4,3,1,2,0:T(8,128)(2,1)}, u32[]{:S(2)}, u32[]{:S(2)}) async-start(bf16[8,26,1,4,32,128]{5,4,3,1,2,0:T(8,128)(2,1)} %fusion.28), calls=%async_computation.2 | async-start | bytes 13631488 | tf_op jit(solution)/shard_map/all_to_all | solution.py:13
  225.1 146.3 %all-to-all-done.2 = bf16[8,26,1,4,32,128]{5,4,3,1,2,0:T(8,128)(2,1)} async-done(((bf16[8,26,1,4,32,128]{5,4,3,1,2,0:T(8,128)(2,1)}), bf16[8,26,1,4,32,128]{5,4,3,1,2,0:T(8,128)(2,1)}, u32[]{:S(2)}, u32[]{:S(2)}) %all-to-all-start.2) | async-done | bytes 6815776 | tf_op jit(solution)/shard_map/all_to_all | solution.py:13
  371.5 3.5 all-to-all-start.1
  375.0 7.9 %copy.49 = bf16[26,8,4,32,128]{4,3,1,0,2:T(8,128)(2,1)} copy(bf16[26,8,4,32,128]{4,3,2,0,1:T(8,128)(2,1)} %bitcast.25) | data formatting | bytes 13631488 | tf_op jit(solution)/shard_map/reshape | solution.py:12
  382.9 5.4 %all-to-all-start.3 = ((bf16[26,8,4,32,128]{4,3,1,0,2:T(8,128)(2,1)}), bf16[26,8,4,32,128]{4,3,1,0,2:T(8,128)(2,1)}, u32[]{:S(2)}, u32[]{:S(2)}) async-start(bf16[26,8,4,32,128]{4,3,1,0,2:T(8,128)(2,1)} %copy.49), calls=%async_computation.3 | async-start | bytes 13631488 | tf_op jit(solution)/shard_map/all_to_all | solution.py:89
  388.3 2.4 slice.25
  392.7 2.1 reshape.120
  394.9 69.7 %all-to-all-done.3 = bf16[26,8,4,32,128]{4,3,1,0,2:T(8,128)(2,1)} async-done(((bf16[26,8,4,32,128]{4,3,1,0,2:T(8,128)(2,1)}), bf16[26,8,4,32,128]{4,3,1,0,2:T(8,128)(2,1)}, u32[]{:S(2)}, u32[]{:S(2)}) %all-to-all-start.3) | async-done | bytes 6815776 | tf_op jit(solution)/shard_map/all_to_all | solution.py:89
  464.6 7.9 %copy.50 = bf16[26,8,4,32,128]{4,3,2,1,0:T(8,128)(2,1)} copy(bf16[26,8,4,32,128]{4,3,1,0,2:T(8,128)(2,1)} %all-to-all-done.3) | data formatting | bytes 13631488 | tf_op jit(solution)/shard_map/all_to_all | solution.py:89
  472.4 66.7 %while.26 = (s32[]{:T(128)}, f32[26,128,128]{2,1,0:T(8,128)}, s32[26,1024]{1,0:T(8,128)}, bf16[26,1024,128]{2,1,0:T(8,128)(2,1)}, s32[]{:T(128)}) while((s32[]{:T(128)}, f32[26,128,128]{2,1,0:T(8,128)}, s32[26,1024]{1,0:T(8,128)}, bf16[26,1024,128]{2,1,0:T(8,128)(2,1)}, s32[]{:T(128)}) %tuple.59), condition=%wide.region_6.7_spmd, body=%wide.region_5.6_spmd.sunk | while | flops 33685504 | bytes 341065 | solution.py:59
  473.2 1.8 fusion.57
  475.8 1.8 fusion.57
  478.3 1.8 fusion.57
  493.7 1.8 fusion.57
  496.3 1.8 fusion.57
  498.8 1.8 fusion.57
  504.0 1.8 fusion.57
  514.2 1.8 fusion.57
  516.8 1.8 fusion.57
  524.5 1.8 fusion.57
  534.7 1.8 fusion.57
  537.3 1.8 fusion.57
  (460 shorter events, 231.6 us)
Async XLA Ops:
  0.6 12.5 %copy-start = (bf16[512,27,128]{2,0,1:T(8,128)(2,1)S(1)}, bf16[512,27,128]{2,0,1:T(8,128)(2,1)}, u32[]{:S(2)}) copy-start(bf16[512,27,128]{2,0,1:T(8,128)(2,1)} %param.9) | copy-start | bytes 10616836
  17.7 3.2 copy-start.2
  196.4 20.1 %all-to-all-start = ((s32[8,1,3328]{2,1,0:T(1,128)}), s32[8,1,3328]{2,1,0:T(1,128)S(1)}, u32[]{:S(2)}, u32[]{:S(2)}) async-start(s32[8,1,3328]{2,1,0:T(1,128)} %reshape.128), calls=%async_computation | async-start | bytes 212992 | tf_op jit(solution)/shard_map/all_to_all | solution.py:91
  203.6 9.0 %copy-start.3 = (bf16[26,1024,128]{2,1,0:T(8,128)(2,1)S(1)}, bf16[26,1024,128]{2,1,0:T(8,128)(2,1)}, u32[]{:S(2)}) copy-start(bf16[26,1024,128]{2,1,0:T(8,128)(2,1)} %get-tuple-element.117) | copy-start | bytes 20447236
  216.5 155.0 %all-to-all-start.2 = ((bf16[8,26,1,4,32,128]{5,4,3,1,2,0:T(8,128)(2,1)}), bf16[8,26,1,4,32,128]{5,4,3,1,2,0:T(8,128)(2,1)}, u32[]{:S(2)}, u32[]{:S(2)}) async-start(bf16[8,26,1,4,32,128]{5,4,3,1,2,0:T(8,128)(2,1)} %fusion.28), calls=%async_computation.2 | async-start | bytes 13631488 | tf_op jit(solution)/shard_map/all_to_all | solution.py:13
  371.5 11.4 %all-to-all-start.1 = ((s32[4,1,6656]{2,1,0:T(1,128)}), s32[4,1,6656]{2,1,0:T(1,128)S(1)}, u32[]{:S(2)}, u32[]{:S(2)}) async-start(s32[4,1,6656]{2,1,0:T(1,128)} %reshape.130), calls=%async_computation.1 | async-start | bytes 212992 | tf_op jit(solution)/shard_map/all_to_all | solution.py:90
  382.9 81.7 %all-to-all-start.3 = ((bf16[26,8,4,32,128]{4,3,1,0,2:T(8,128)(2,1)}), bf16[26,8,4,32,128]{4,3,1,0,2:T(8,128)(2,1)}, u32[]{:S(2)}, u32[]{:S(2)}) async-start(bf16[26,8,4,32,128]{4,3,1,0,2:T(8,128)(2,1)} %copy.49), calls=%async_computation.3 | async-start | bytes 13631488 | tf_op jit(solution)/shard_map/all_to_all | solution.py:89
  392.7 146.4 %copy-start.1 = (bf16[512,27,128]{2,0,1:T(8,128)(2,1)S(1)}, bf16[512,27,128]{2,0,1:T(8,128)(2,1)}, u32[]{:S(2)}) copy-start(bf16[512,27,128]{2,0,1:T(8,128)(2,1)} %param.9) | copy-start | bytes 10616836
